TPU v7x, 256 devices: a whole 4x4x8 slice. The times are simulated.
256 devices in a mesh: vox: 64 (over x, z_lo, y, core), load: 4 (over z_hi).
Axes of the slice: x: 4, y: 4, z: 8 (z_hi: 4, z_lo: 2; z = z_hi * 2 + z_lo), core: 2. Of those that a mesh axis runs over, the one named last changes fastest.
Arguments:
- reduced_shape_matrix: bfloat16 [65536, 512], P('vox'), may hold values from -0.25 to 0.25
- young_modulus: float32 [65536], P('vox'), may hold values from 0.5 to 2
- work_stiffening_modulus: float32 [65536], P('vox'), may hold values from 0.2 to 2
- entry_flow_stress: float32 [65536], P('vox'), may hold values from 0.5 to 2
- dilation_factor: float32 [65536], P('vox'), may hold values from 0.5 to 2
- heat_difference: float32 [512], P('load'), may hold values from -4 to 4
- flowing_entry_flags: int32 [65536, 512], P('vox', 'load'), may hold values 0 or 1
- starting_permanent_deformation: float32 [65536, 512], P('vox', 'load'), may hold values from -3 to 3
- starting_weights: float32 [512, 512], P('vox', 'load'), may hold values from -5 to 5
- applied_reduced_vector: float32 [512, 512], P('vox', 'load'), may hold values from -768 to 768
- approx_tangent_inverse: float32 [512, 512], replicated, as said below
Outputs:
- final_mode_coefficients: float32 [512, 512], P('vox', 'load')
- strain_out: float32 [65536, 512], P('vox', 'load')
Inputs may be any that keep to these rules, and one draw needn't show every extreme that they name: `approx_tangent_inverse`: it has a positive diagonal.
All inputs are finite; a program needn't handle non-finite values. No bound on the sum of `flowing_entry_flags` on one device may be relied on, other than what follows from the above.
Results may differ from a plain program's by a relative error of at most 0.0013.
Values may be sent and summed in bfloat16 or wider, within the bound.
No kernel may reach another device: no remote copies, remote signals or barrier semaphores. Data moves between devices by JAX's collectives and lax.ppermute only.
A program may use at most 64 MiB of HBM per device.

v0:
```python
import jax
import jax.numpy as jnp
from jax import lax
from jax.sharding import Mesh
from jax.sharding import PartitionSpec as P

M = 512
ITERS = 3
VOX = ("vox_0", "vox_1", "vox_2", "vox_3")
VOX_LOAD = ("vox_0", "vox_1", "vox_2", "vox_3", "load")


def joined_along(pieces, dim):
    pieces = jnp.moveaxis(pieces, 0, dim)
    shape = pieces.shape
    return pieces.reshape(*shape[:dim], shape[dim] * shape[dim + 1], *shape[dim + 2 :])


def from_everyone(shard, axis):
    size = lax.axis_size(axis)
    return lax.all_to_all(
        jnp.broadcast_to(shard[None], (size, *shard.shape)), axis, 0, 0, tiled=True
    )


def collect(shard, axis, dim):
    return joined_along(from_everyone(shard, axis), dim)


def in_blocks(shard, dim, size):
    before, after = (shard.shape[:dim], shard.shape[dim + 1 :])
    return jnp.moveaxis(shard.reshape(*before, size, -1, *after), dim, 0)


def sum_at_owner(shard, axis, dim):
    size = lax.axis_size(axis)
    pieces = lax.all_to_all(in_blocks(shard, dim, size), axis, 0, 0, tiled=True)
    return jnp.sum(pieces, axis=0)


def over_axes(shard, axes):
    for axis in axes:
        shard = lax.psum(shard, axis)
    return shard


def shards(
    reduced_shape_matrix,
    young_modulus,
    work_stiffening_modulus,
    entry_flow_stress,
    dilation_factor,
    heat_difference,
    flowing_entry_flags,
    starting_permanent_deformation,
    starting_weights,
    applied_reduced_vector,
    approx_tangent_inverse,
):
    own_rows = starting_weights.shape[0]
    points = starting_weights.shape[1]
    load_point_total = points * lax.axis_size("load")
    plastic = starting_permanent_deformation
    active = flowing_entry_flags.astype(jnp.float32)
    modulus = young_modulus[:, None]
    harden = work_stiffening_modulus[:, None]
    yielded = entry_flow_stress[:, None]
    heating_history = dilation_factor[:, None] * heat_difference[None, :]
    xi_now = starting_weights
    my_precond = lax.dynamic_slice_in_dim(
        approx_tangent_inverse, lax.axis_index(VOX) * own_rows, own_rows, 0
    )
    for sweep in range(ITERS):
        xi_whole = collect(xi_now.astype(jnp.bfloat16), VOX, 0)
        strain = jnp.dot(reduced_shape_matrix, xi_whole, preferred_element_type=jnp.float32)
        trial = modulus * (strain - heating_history - plastic)
        excess = trial - yielded * jnp.tanh(trial / yielded)
        increment = active * excess / (modulus + harden)
        stress = (trial - modulus * increment).astype(jnp.bfloat16)
        stress, plastic = (stress, plastic + increment)
        partial_sum = lax.dot_general(
            reduced_shape_matrix,
            stress,
            (((0,), (0,)), ((), ())),
            preferred_element_type=jnp.float32,
        )
        resid = sum_at_owner(partial_sum, VOX, 0) - applied_reduced_vector
        resid_all = collect(resid, VOX, 0)
        delta = jnp.dot(my_precond, resid_all, precision=lax.Precision.HIGHEST)
        spread = over_axes(jnp.sum(delta * delta), VOX_LOAD) / (M * load_point_total)
        xi_now = xi_now - delta / (1.0 + spread)
    return (xi_now, plastic)


def solution(mesh):
    split = Mesh(
        mesh.devices.reshape(4, 2, 4, 2, mesh.shape["load"]),
        ("vox_0", "vox_1", "vox_2", "vox_3", "load"),
    )
    return jax.shard_map(
        shards,
        mesh=split,
        in_specs=(
            P(VOX, None),
            P(VOX),
            P(VOX),
            P(VOX),
            P(VOX),
            P("load"),
            P(VOX, "load"),
            P(VOX, "load"),
            P(VOX, "load"),
            P(VOX, "load"),
            P(),
        ),
        out_specs=(P(VOX, "load"), P(VOX, "load")),
        check_vma=False,
    )
```

profile of v0, /device:TPU:2, one launch (start us, length us, event | category | flops | bytes accessed | tf_op | source)
XLA Modules:
  0.0 264.1 jit_solution(17287310911029910719)
XLA Ops:
  2.1 9.5 %all-to-all-start = ((bf16[64,8,128]{2,1,0:T(8,128)(2,1)}), bf16[64,8,128]{2,1,0:T(8,128)(2,1)S(1)}, u32[]{:S(2)}, u32[]{:S(2)}) async-start(bf16[64,8,128]{2,1,0:T(8,128)(2,1)} %broadcast_in_dim.12), calls=%async_computation | async-start | bytes 262144 | tf_op jit(solution)/shard_map/all_to_all | solution.py:21
  11.7 7.4 %all-to-all-done = bf16[64,8,128]{2,1,0:T(8,128)(2,1)S(1)} async-done(((bf16[64,8,128]{2,1,0:T(8,128)(2,1)}), bf16[64,8,128]{2,1,0:T(8,128)(2,1)S(1)}, u32[]{:S(2)}, u32[]{:S(2)}) %all-to-all-start) | async-done | bytes 131104 | tf_op jit(solution)/shard_map/all_to_all | solution.py:21
  21.6 14.0 %all_to_all.45 = f32[64,8,128]{2,1,0:T(8,128)S(1)} all-to-all(f32[64,8,128]{2,1,0:T(8,128)S(1)} %bitcast.57), channel_id=1, replica_groups=mesh['vox_0'=4,'vox_1'=2,'vox_2'=4,'vox_3'=2,'load'=4] {'vox_0','vox_1',..., dimensions={0} | all-to-all | bytes 524288 | tf_op jit(solution)/shard_map/all_to_all | solution.py:37
  37.1 5.7 %all-to-all-start.2 = ((f32[64,8,128]{2,1,0:T(8,128)}), f32[64,8,128]{2,1,0:T(8,128)S(1)}, u32[]{:S(2)}, u32[]{:S(2)}) async-start(f32[64,8,128]{2,1,0:T(8,128)} %broadcast_in_dim.13), calls=%async_computation.2 | async-start | bytes 524288 | tf_op jit(solution)/shard_map/all_to_all | solution.py:21
  42.8 8.8 %all-to-all-done.2 = f32[64,8,128]{2,1,0:T(8,128)S(1)} async-done(((f32[64,8,128]{2,1,0:T(8,128)}), f32[64,8,128]{2,1,0:T(8,128)S(1)}, u32[]{:S(2)}, u32[]{:S(2)}) %all-to-all-start.2) | async-done | bytes 262176 | tf_op jit(solution)/shard_map/all_to_all | solution.py:21
  53.1 9.7 %psum.105 = f32[]{:T(128)} all-reduce(f32[]{:T(128)} %get-tuple-element.4), channel_id=1, replica_groups=mesh['vox_0'=4,'vox_1'=2,'vox_2'=4,'vox_3'=2,'load'=4] {'vox_0'}, use_global_device_ids=true, to_apply=%region_2.0 | all-reduce | flops 1 | bytes 8 | tf_op jit(solution)/shard_map/psum | solution.py:43
  62.8 5.5 %psum.106 = f32[]{:T(128)} all-reduce(f32[]{:T(128)} %psum.105), channel_id=1, replica_groups=mesh['vox_0'=4,'vox_1'=2,'vox_2'=4,'vox_3'=2,'load'=4] {'vox_1'}, use_global_device_ids=true, to_apply=%region_3.0 | all-reduce | flops 1 | bytes 8 | tf_op jit(solution)/shard_map/psum | solution.py:43
  68.4 9.5 %psum.107 = f32[]{:T(128)} all-reduce(f32[]{:T(128)} %psum.106), channel_id=1, replica_groups=mesh['vox_0'=4,'vox_1'=2,'vox_2'=4,'vox_3'=2,'load'=4] {'vox_2'}, use_global_device_ids=true, to_apply=%region_4.0 | all-reduce | flops 1 | bytes 8 | tf_op jit(solution)/shard_map/psum | solution.py:43
  77.9 3.1 %psum.108 = f32[]{:T(128)} all-reduce(f32[]{:T(128)} %psum.107), channel_id=1, replica_groups=mesh['vox_0'=4,'vox_1'=2,'vox_2'=4,'vox_3'=2,'load'=4] {'vox_3'}, use_global_device_ids=true, to_apply=%region_5.0 | all-reduce | flops 1 | bytes 8 | tf_op jit(solution)/shard_map/psum | solution.py:43
  81.0 14.6 %psum.109 = f32[]{:T(128)} all-reduce(f32[]{:T(128)} %psum.108), channel_id=1, replica_groups=mesh['vox_0'=4,'vox_1'=2,'vox_2'=4,'vox_3'=2,'load'=4] {'load'}, use_global_device_ids=true, to_apply=%region_6.0 | all-reduce | flops 1 | bytes 8 | tf_op jit(solution)/shard_map/psum | solution.py:43
  96.3 11.9 %all_to_all.46 = bf16[64,8,128]{2,1,0:T(8,128)(2,1)S(1)} all-to-all(bf16[64,8,128]{2,1,0:T(8,128)(2,1)S(1)} %broadcast_in_dim.14), channel_id=1, replica_groups=mesh['vox_0'=4,'vox_1'=2,'vox_2'=4,'vox_3'=2,'load'=4] {'vox_0','vox_1',..., dimensions={0} | all-to-all | bytes 262144 | tf_op jit(solution)/shard_map/all_to_all | solution.py:21
  110.7 14.0 %all_to_all.47 = f32[64,8,128]{2,1,0:T(8,128)S(1)} all-to-all(f32[64,8,128]{2,1,0:T(8,128)S(1)} %bitcast.58), channel_id=1, replica_groups=mesh['vox_0'=4,'vox_1'=2,'vox_2'=4,'vox_3'=2,'load'=4] {'vox_0','vox_1',..., dimensions={0} | all-to-all | bytes 524288 | tf_op jit(solution)/shard_map/all_to_all | solution.py:37
  124.8 14.2 %all_to_all.48 = f32[64,8,128]{2,1,0:T(8,128)S(1)} all-to-all(f32[64,8,128]{2,1,0:T(8,128)S(1)} %broadcast_in_dim.15), channel_id=1, replica_groups=mesh['vox_0'=4,'vox_1'=2,'vox_2'=4,'vox_3'=2,'load'=4] {'vox_0','vox_1',..., dimensions={0} | all-to-all | bytes 524288 | tf_op jit(solution)/shard_map/all_to_all | solution.py:21
  140.6 9.7 %psum.110 = f32[]{:T(128)} all-reduce(f32[]{:T(128)} %get-tuple-element.6), channel_id=1, replica_groups=mesh['vox_0'=4,'vox_1'=2,'vox_2'=4,'vox_3'=2,'load'=4] {'vox_0'}, use_global_device_ids=true, to_apply=%region_9.0 | all-reduce | flops 1 | bytes 8 | tf_op jit(solution)/shard_map/psum | solution.py:43
  150.3 5.5 %psum.111 = f32[]{:T(128)} all-reduce(f32[]{:T(128)} %psum.110), channel_id=1, replica_groups=mesh['vox_0'=4,'vox_1'=2,'vox_2'=4,'vox_3'=2,'load'=4] {'vox_1'}, use_global_device_ids=true, to_apply=%region_10.0 | all-reduce | flops 1 | bytes 8 | tf_op jit(solution)/shard_map/psum | solution.py:43
  155.8 9.5 %psum.112 = f32[]{:T(128)} all-reduce(f32[]{:T(128)} %psum.111), channel_id=1, replica_groups=mesh['vox_0'=4,'vox_1'=2,'vox_2'=4,'vox_3'=2,'load'=4] {'vox_2'}, use_global_device_ids=true, to_apply=%region_11.0 | all-reduce | flops 1 | bytes 8 | tf_op jit(solution)/shard_map/psum | solution.py:43
  168.4 10.7 %psum.114 = f32[]{:T(128)} all-reduce(f32[]{:T(128)} %psum.113), channel_id=1, replica_groups=mesh['vox_0'=4,'vox_1'=2,'vox_2'=4,'vox_3'=2,'load'=4] {'load'}, use_global_device_ids=true, to_apply=%region_13.0 | all-reduce | flops 1 | bytes 8 | tf_op jit(solution)/shard_map/psum | solution.py:43
  179.8 11.9 %all_to_all.49 = bf16[64,8,128]{2,1,0:T(8,128)(2,1)S(1)} all-to-all(bf16[64,8,128]{2,1,0:T(8,128)(2,1)S(1)} %broadcast_in_dim.16), channel_id=1, replica_groups=mesh['vox_0'=4,'vox_1'=2,'vox_2'=4,'vox_3'=2,'load'=4] {'vox_0','vox_1',..., dimensions={0} | all-to-all | bytes 262144 | tf_op jit(solution)/shard_map/all_to_all | solution.py:21
  194.5 14.0 %all_to_all.50 = f32[64,8,128]{2,1,0:T(8,128)S(1)} all-to-all(f32[64,8,128]{2,1,0:T(8,128)S(1)} %bitcast.59), channel_id=1, replica_groups=mesh['vox_0'=4,'vox_1'=2,'vox_2'=4,'vox_3'=2,'load'=4] {'vox_0','vox_1',..., dimensions={0} | all-to-all | bytes 524288 | tf_op jit(solution)/shard_map/all_to_all | solution.py:37
  208.6 14.1 %all_to_all.51 = f32[64,8,128]{2,1,0:T(8,128)S(1)} all-to-all(f32[64,8,128]{2,1,0:T(8,128)S(1)} %broadcast_in_dim.17), channel_id=1, replica_groups=mesh['vox_0'=4,'vox_1'=2,'vox_2'=4,'vox_3'=2,'load'=4] {'vox_0','vox_1',..., dimensions={0} | all-to-all | bytes 524288 | tf_op jit(solution)/shard_map/all_to_all | solution.py:21
  224.3 9.7 %psum.115 = f32[]{:T(128)} all-reduce(f32[]{:T(128)} %get-tuple-element.8), channel_id=1, replica_groups=mesh['vox_0'=4,'vox_1'=2,'vox_2'=4,'vox_3'=2,'load'=4] {'vox_0'}, use_global_device_ids=true, to_apply=%region_16.0 | all-reduce | flops 1 | bytes 8 | tf_op jit(solution)/shard_map/psum | solution.py:43
  234.0 5.5 %psum.116 = f32[]{:T(128)} all-reduce(f32[]{:T(128)} %psum.115), channel_id=1, replica_groups=mesh['vox_0'=4,'vox_1'=2,'vox_2'=4,'vox_3'=2,'load'=4] {'vox_1'}, use_global_device_ids=true, to_apply=%region_17.0 | all-reduce | flops 1 | bytes 8 | tf_op jit(solution)/shard_map/psum | solution.py:43
  239.5 9.5 %psum.117 = f32[]{:T(128)} all-reduce(f32[]{:T(128)} %psum.116), channel_id=1, replica_groups=mesh['vox_0'=4,'vox_1'=2,'vox_2'=4,'vox_3'=2,'load'=4] {'vox_2'}, use_global_device_ids=true, to_apply=%region_18.0 | all-reduce | flops 1 | bytes 8 | tf_op jit(solution)/shard_map/psum | solution.py:43
  252.1 10.7 %psum.119 = f32[]{:T(128)} all-reduce(f32[]{:T(128)} %psum.118), channel_id=1, replica_groups=mesh['vox_0'=4,'vox_1'=2,'vox_2'=4,'vox_3'=2,'load'=4] {'load'}, use_global_device_ids=true, to_apply=%region_20.0 | all-reduce | flops 1 | bytes 8 | tf_op jit(solution)/shard_map/psum | solution.py:43
  (55 shorter events, 22.3 us)
Async XLA Ops:
  0.6 18.5 %copy-start = (bf16[1024,512]{1,0:T(8,128)(2,1)S(1)}, bf16[1024,512]{1,0:T(8,128)(2,1)}, u32[]{:S(2)}) copy-start(bf16[1024,512]{1,0:T(8,128)(2,1)} %param.11) | copy-start | bytes 3145732
  2.1 9.5 %copy-start.4 = (f32[1024]{0:T(1024)S(1)}, f32[1024]{0:T(1024)}, u32[]{:S(2)}) copy-start(f32[1024]{0:T(1024)} %param.12) | copy-start | bytes 12292
  2.1 9.5 %copy-start.6 = (f32[1024]{0:T(1024)S(1)}, f32[1024]{0:T(1024)}, u32[]{:S(2)}) copy-start(f32[1024]{0:T(1024)} %param.13) | copy-start | bytes 12292
  2.1 17.0 %all-to-all-start = ((bf16[64,8,128]{2,1,0:T(8,128)(2,1)}), bf16[64,8,128]{2,1,0:T(8,128)(2,1)S(1)}, u32[]{:S(2)}, u32[]{:S(2)}) async-start(bf16[64,8,128]{2,1,0:T(8,128)(2,1)} %broadcast_in_dim.12), calls=%async_computation | async-start | bytes 262144 | tf_op jit(solution)/shard_map/all_to_all | solution.py:21
  11.6 7.5 %copy-start.5 = (f32[1024]{0:T(1024)S(1)}, f32[1024]{0:T(1024)}, u32[]{:S(2)}) copy-start(f32[1024]{0:T(1024)} %param.15) | copy-start | bytes 12292
  11.7 7.5 %copy-start.7 = (f32[128]{0:T(128)S(1)}, f32[128]{0:T(128)}, u32[]{:S(2)}) copy-start(f32[128]{0:T(128)} %param.16) | copy-start | bytes 1540
  11.7 8.9 %copy-start.8 = (s32[1024,128]{1,0:T(8,128)S(1)}, s32[1024,128]{1,0:T(8,128)}, u32[]{:S(2)}) copy-start(s32[1024,128]{1,0:T(8,128)} %param.17) | copy-start | bytes 1572868
  11.7 8.9 %copy-start.9 = (f32[1024]{0:T(1024)S(1)}, f32[1024]{0:T(1024)}, u32[]{:S(2)}) copy-start(f32[1024]{0:T(1024)} %param.14) | copy-start | bytes 12292
  35.7 0.7 copy-start.2
  37.1 71.1 %copy-start.1 = (f32[1024,128]{1,0:T(8,128)S(1)}, f32[1024,128]{1,0:T(8,128)}, u32[]{:S(2)}) copy-start(f32[1024,128]{1,0:T(8,128)} %param.18) | copy-start | bytes 1572868
  37.1 14.5 %all-to-all-start.2 = ((f32[64,8,128]{2,1,0:T(8,128)}), f32[64,8,128]{2,1,0:T(8,128)S(1)}, u32[]{:S(2)}, u32[]{:S(2)}) async-start(f32[64,8,128]{2,1,0:T(8,128)} %broadcast_in_dim.13), calls=%async_computation.2 | async-start | bytes 524288 | tf_op jit(solution)/shard_map/all_to_all | solution.py:21
  81.0 15.3 %copy-start.3 = (f32[8,128]{1,0:T(8,128)S(1)}, f32[8,128]{1,0:T(8,128)}, u32[]{:S(2)}) copy-start(f32[8,128]{1,0:T(8,128)} %param.19) | copy-start | bytes 12292
  108.9 0.8 copy-start.10
  124.8 66.9 %copy-start.11 = (f32[1024,128]{1,0:T(8,128)S(1)}, f32[1024,128]{1,0:T(8,128)}, u32[]{:S(2)}) copy-start(f32[1024,128]{1,0:T(8,128)} %copy-done.10) | copy-start | bytes 1572868
where the time goes:
time: 265 us; the launch traced here: 264 us
  blocking collectives  214 us (81%)
  waiting for transfers between devices  16.2 us (6%)
  starting transfers between devices  15.2 us (6%)
  matrix products  11.2 us (4%)
  local copies, waits for them, and re-layouts  3.32 us (1%)
  between operations  2.83 us (1%)
    psum x15, blocking collectives, over_axes(): shard = lax.psum(shard, axis)  119 us
    all_to_all x4, blocking collectives, from_everyone(): lax.all_to_all(jnp.broadcast_to(shard[None], (size, *shard.shape)), axis,...  52.2 us
    all_to_all x3, blocking collectives, sum_at_owner(): pieces = lax.all_to_all(in_blocks(shard, dim, size), axis, 0, 0, tiled=True)  42.1 us
    all_to_all x2, waiting for transfers between devices, from_everyone(): lax.all_to_all(jnp.broadcast_to(shard[None], (size, *shard.shape)), axis,...  16.2 us
    all_to_all x2, starting transfers between devices, from_everyone(): lax.all_to_all(jnp.broadcast_to(shard[None], (size, *shard.shape)), axis,...  15.2 us
  transfers between devices with their start and end apart: 2, of which 2 were waited for; matrix products, arithmetic and copies ran while one was open for 0% of the time, Pallas kernels for 0%

commit v1 on v0

--- a/solution.py
+++ b/solution.py
@@ -8,6 +8,11 @@
 ITERS = 3
 VOX = ("vox_0", "vox_1", "vox_2", "vox_3")
 VOX_LOAD = ("vox_0", "vox_1", "vox_2", "vox_3", "load")
+
+
+def watch_plane(chip_axis, unit):
+    w1 = lax.all_gather(unit, axis_name=chip_axis).sum(axis=0)
+    return w1
 
 
 def joined_along(pieces, dim):
@@ -40,7 +45,7 @@
 
 def over_axes(shard, axes):
     for axis in axes:
-        shard = lax.psum(shard, axis)
+        shard = watch_plane(axis, shard)
     return shard
 
 

time: 265 us -> 289 us (1.091)
  blocking collectives: 214 us -> 190 us
  local copies, waits for them, and re-layouts: 3.32 us -> 27.3 us
  other arithmetic: 1.63 us -> 10.7 us
  waiting for transfers between devices: 16.2 us -> 24.4 us
  starting transfers between devices: 15.2 us -> 20.7 us
    psum x15 -> x0, blocking collectives: 119 us -> none  [over_axes(): shard = lax.psum(shard, axis)]
    unnamed x0 -> x15, blocking collectives: none -> 110 us
    unnamed x24 -> x69, local copies, waits for them, and re-layouts: 1.46 us -> 24.7 us
    all_to_all x3 -> x2, blocking collectives: 42.1 us -> 28.1 us  [sum_at_owner(): pieces = lax.all_to_all(in_blocks(shard, dim, size), axis, 0, 0, tiled=True)]
    reduce_sum x0 -> x15, other arithmetic: none -> 9.05 us  [watch_plane(): w1 = lax.all_gather(unit, axis_name=chip_axis).sum(axis=0)]
    all_to_all x0 -> x1, waiting for transfers between devices: none -> 8.83 us  [sum_at_owner(): pieces = lax.all_to_all(in_blocks(shard, dim, size), axis, 0, 0, tiled=True)]
    all_to_all x0 -> x1, starting transfers between devices: none -> 5.55 us  [sum_at_owner(): pieces = lax.all_to_all(in_blocks(shard, dim, size), axis, 0, 0, tiled=True)]
  transfers between devices with their start and end apart: 2 -> 3, of which waited for: 2 -> 3; matrix products, arithmetic and copies ran while one was open for 0% -> 0% of each run, Pallas kernels for 0% -> 0%
where the time goes in v1:
time: 289 us; the launch traced here: 288 us
  blocking collectives  190 us (66%)
  local copies, waits for them, and re-layouts  27.3 us (9%)
  waiting for transfers between devices  24.4 us (8%)
  starting transfers between devices  20.7 us (7%)
  matrix products  11.2 us (4%)
  other arithmetic  10.7 us (4%)
  between operations  2.91 us (1%)
    unnamed x15, blocking collectives  110 us
    all_to_all x4, blocking collectives, from_everyone(): lax.all_to_all(jnp.broadcast_to(shard[None], (size, *shard.shape)), axis,...  52.2 us
    all_to_all x2, blocking collectives, sum_at_owner(): pieces = lax.all_to_all(in_blocks(shard, dim, size), axis, 0, 0, tiled=True)  28.1 us
    unnamed x69, local copies, waits for them, and re-layouts  24.7 us
    all_to_all x2, waiting for transfers between devices, from_everyone(): lax.all_to_all(jnp.broadcast_to(shard[None], (size, *shard.shape)), axis,...  15.6 us
    all_to_all x2, starting transfers between devices, from_everyone(): lax.all_to_all(jnp.broadcast_to(shard[None], (size, *shard.shape)), axis,...  15.2 us
    reduce_sum x15, other arithmetic, watch_plane(): w1 = lax.all_gather(unit, axis_name=chip_axis).sum(axis=0)  9.05 us
    all_to_all x1, waiting for transfers between devices, sum_at_owner(): pieces = lax.all_to_all(in_blocks(shard, dim, size), axis, 0, 0, tiled=True)  8.83 us
  transfers between devices with their start and end apart: 3, of which 3 were waited for; matrix products, arithmetic and copies ran while one was open for 0% of the time, Pallas kernels for 0%

profile of v1, /device:TPU:2, one launch (start us, length us, event | category | flops | bytes accessed | tf_op | source)
XLA Modules:
  0.0 287.5 jit_solution(10634000545804459388)
XLA Ops:
  2.1 9.5 %all-to-all-start = ((bf16[64,8,128]{2,1,0:T(8,128)(2,1)}), bf16[64,8,128]{2,1,0:T(8,128)(2,1)S(1)}, u32[]{:S(2)}, u32[]{:S(2)}) async-start(bf16[64,8,128]{2,1,0:T(8,128)(2,1)} %broadcast_in_dim.12), calls=%async_computation | async-start | bytes 262144 | tf_op jit(solution)/shard_map/all_to_all | solution.py:26
  11.7 7.4 %all-to-all-done = bf16[64,8,128]{2,1,0:T(8,128)(2,1)S(1)} async-done(((bf16[64,8,128]{2,1,0:T(8,128)(2,1)}), bf16[64,8,128]{2,1,0:T(8,128)(2,1)S(1)}, u32[]{:S(2)}, u32[]{:S(2)}) %all-to-all-start) | async-done | bytes 131104 | tf_op jit(solution)/shard_map/all_to_all | solution.py:26
  22.3 5.5 %all-to-all-start.1 = ((f32[64,8,128]{2,1,0:T(8,128)}), f32[64,8,128]{2,1,0:T(8,128)S(1)}, u32[]{:S(2)}, u32[]{:S(2)}) async-start(f32[64,8,128]{2,1,0:T(8,128)} %bitcast.2), calls=%async_computation.1 | async-start | bytes 524288 | tf_op jit(solution)/shard_map/all_to_all | solution.py:42
  27.9 8.8 %all-to-all-done.1 = f32[64,8,128]{2,1,0:T(8,128)S(1)} async-done(((f32[64,8,128]{2,1,0:T(8,128)}), f32[64,8,128]{2,1,0:T(8,128)S(1)}, u32[]{:S(2)}, u32[]{:S(2)}) %all-to-all-start.1) | async-done | bytes 262176 | tf_op jit(solution)/shard_map/all_to_all | solution.py:42
  37.6 5.7 %all-to-all-start.2 = ((f32[64,8,128]{2,1,0:T(8,128)}), f32[64,8,128]{2,1,0:T(8,128)S(1)}, u32[]{:S(2)}, u32[]{:S(2)}) async-start(f32[64,8,128]{2,1,0:T(8,128)} %broadcast_in_dim.13), calls=%async_computation.2 | async-start | bytes 524288 | tf_op jit(solution)/shard_map/all_to_all | solution.py:26
  44.0 8.1 %all-to-all-done.2 = f32[64,8,128]{2,1,0:T(8,128)S(1)} async-done(((f32[64,8,128]{2,1,0:T(8,128)}), f32[64,8,128]{2,1,0:T(8,128)S(1)}, u32[]{:S(2)}, u32[]{:S(2)}) %all-to-all-start.2) | async-done | bytes 262176 | tf_op jit(solution)/shard_map/all_to_all | solution.py:26
  55.7 9.1 %all-reduce = f32[4]{0:T(128)S(1)} all-reduce(f32[4]{0:T(128)S(1)} %dynamic-update-slice), channel_id=1, replica_groups=mesh['vox_0'=4,'vox_1'=2,'vox_2'=4,'vox_3'=2,'load'=4] {'vox_0'}, use_global_device_ids=true, to_apply=%add | all-reduce | flops 4 | bytes 32
  67.3 4.9 %all-reduce.1 = f32[2]{0:T(128)S(1)} all-reduce(f32[2]{0:T(128)S(1)} %dynamic-update-slice.1), channel_id=1, replica_groups=mesh['vox_0'=4,'vox_1'=2,'vox_2'=4,'vox_3'=2,'load'=4] {'vox_1'}, use_global_device_ids=true, to_apply=%add.1 | all-reduce | flops 2 | bytes 16
  74.8 8.9 %all-reduce.2 = f32[4]{0:T(128)S(1)} all-reduce(f32[4]{0:T(128)S(1)} %dynamic-update-slice.2), channel_id=1, replica_groups=mesh['vox_0'=4,'vox_1'=2,'vox_2'=4,'vox_3'=2,'load'=4] {'vox_2'}, use_global_device_ids=true, to_apply=%add.2 | all-reduce | flops 4 | bytes 32
  90.7 14.0 %all-reduce.4 = f32[4]{0:T(128)S(1)} all-reduce(f32[4]{0:T(128)S(1)} %dynamic-update-slice.4), channel_id=1, replica_groups=mesh['vox_0'=4,'vox_1'=2,'vox_2'=4,'vox_3'=2,'load'=4] {'load'}, use_global_device_ids=true, to_apply=%add.4 | all-reduce | flops 4 | bytes 32
  106.0 11.9 %all_to_all.45 = bf16[64,8,128]{2,1,0:T(8,128)(2,1)S(1)} all-to-all(bf16[64,8,128]{2,1,0:T(8,128)(2,1)S(1)} %broadcast_in_dim.14), channel_id=1, replica_groups=mesh['vox_0'=4,'vox_1'=2,'vox_2'=4,'vox_3'=2,'load'=4] {'vox_0','vox_1',..., dimensions={0} | all-to-all | bytes 262144 | tf_op jit(solution)/shard_map/all_to_all | solution.py:26
  120.4 14.0 %all_to_all.49 = f32[64,8,128]{2,1,0:T(8,128)S(1)} all-to-all(f32[64,8,128]{2,1,0:T(8,128)S(1)} %bitcast.77), channel_id=1, replica_groups=mesh['vox_0'=4,'vox_1'=2,'vox_2'=4,'vox_3'=2,'load'=4] {'vox_0','vox_1',..., dimensions={0} | all-to-all | bytes 524288 | tf_op jit(solution)/shard_map/all_to_all | solution.py:42
  134.5 14.2 %all_to_all.46 = f32[64,8,128]{2,1,0:T(8,128)S(1)} all-to-all(f32[64,8,128]{2,1,0:T(8,128)S(1)} %broadcast_in_dim.15), channel_id=1, replica_groups=mesh['vox_0'=4,'vox_1'=2,'vox_2'=4,'vox_3'=2,'load'=4] {'vox_0','vox_1',..., dimensions={0} | all-to-all | bytes 524288 | tf_op jit(solution)/shard_map/all_to_all | solution.py:26
  151.8 9.1 %all-reduce.5 = f32[4]{0:T(128)S(1)} all-reduce(f32[4]{0:T(128)S(1)} %dynamic-update-slice.5), channel_id=1, replica_groups=mesh['vox_0'=4,'vox_1'=2,'vox_2'=4,'vox_3'=2,'load'=4] {'vox_0'}, use_global_device_ids=true, to_apply=%add.5 | all-reduce | flops 4 | bytes 32
  162.8 4.9 %all-reduce.6 = f32[2]{0:T(128)S(1)} all-reduce(f32[2]{0:T(128)S(1)} %dynamic-update-slice.6), channel_id=1, replica_groups=mesh['vox_0'=4,'vox_1'=2,'vox_2'=4,'vox_3'=2,'load'=4] {'vox_1'}, use_global_device_ids=true, to_apply=%add.6 | all-reduce | flops 2 | bytes 16
  169.7 8.9 %all-reduce.7 = f32[4]{0:T(128)S(1)} all-reduce(f32[4]{0:T(128)S(1)} %dynamic-update-slice.7), channel_id=1, replica_groups=mesh['vox_0'=4,'vox_1'=2,'vox_2'=4,'vox_3'=2,'load'=4] {'vox_2'}, use_global_device_ids=true, to_apply=%add.7 | all-reduce | flops 4 | bytes 32
  184.9 10.2 %all-reduce.9 = f32[4]{0:T(128)S(1)} all-reduce(f32[4]{0:T(128)S(1)} %dynamic-update-slice.9), channel_id=1, replica_groups=mesh['vox_0'=4,'vox_1'=2,'vox_2'=4,'vox_3'=2,'load'=4] {'load'}, use_global_device_ids=true, to_apply=%add.9 | all-reduce | flops 4 | bytes 32
  196.5 11.9 %all_to_all.47 = bf16[64,8,128]{2,1,0:T(8,128)(2,1)S(1)} all-to-all(bf16[64,8,128]{2,1,0:T(8,128)(2,1)S(1)} %broadcast_in_dim.16), channel_id=1, replica_groups=mesh['vox_0'=4,'vox_1'=2,'vox_2'=4,'vox_3'=2,'load'=4] {'vox_0','vox_1',..., dimensions={0} | all-to-all | bytes 262144 | tf_op jit(solution)/shard_map/all_to_all | solution.py:26
  211.2 14.0 %all_to_all.50 = f32[64,8,128]{2,1,0:T(8,128)S(1)} all-to-all(f32[64,8,128]{2,1,0:T(8,128)S(1)} %bitcast.78), channel_id=1, replica_groups=mesh['vox_0'=4,'vox_1'=2,'vox_2'=4,'vox_3'=2,'load'=4] {'vox_0','vox_1',..., dimensions={0} | all-to-all | bytes 524288 | tf_op jit(solution)/shard_map/all_to_all | solution.py:42
  225.3 14.1 %all_to_all.48 = f32[64,8,128]{2,1,0:T(8,128)S(1)} all-to-all(f32[64,8,128]{2,1,0:T(8,128)S(1)} %broadcast_in_dim.17), channel_id=1, replica_groups=mesh['vox_0'=4,'vox_1'=2,'vox_2'=4,'vox_3'=2,'load'=4] {'vox_0','vox_1',..., dimensions={0} | all-to-all | bytes 524288 | tf_op jit(solution)/shard_map/all_to_all | solution.py:26
  242.4 9.1 %all-reduce.10 = f32[4]{0:T(128)S(1)} all-reduce(f32[4]{0:T(128)S(1)} %dynamic-update-slice.10), channel_id=1, replica_groups=mesh['vox_0'=4,'vox_1'=2,'vox_2'=4,'vox_3'=2,'load'=4] {'vox_0'}, use_global_device_ids=true, to_apply=%add.10 | all-reduce | flops 4 | bytes 32
  253.4 4.9 %all-reduce.11 = f32[2]{0:T(128)S(1)} all-reduce(f32[2]{0:T(128)S(1)} %dynamic-update-slice.11), channel_id=1, replica_groups=mesh['vox_0'=4,'vox_1'=2,'vox_2'=4,'vox_3'=2,'load'=4] {'vox_1'}, use_global_device_ids=true, to_apply=%add.11 | all-reduce | flops 2 | bytes 16
  260.3 8.9 %all-reduce.12 = f32[4]{0:T(128)S(1)} all-reduce(f32[4]{0:T(128)S(1)} %dynamic-update-slice.12), channel_id=1, replica_groups=mesh['vox_0'=4,'vox_1'=2,'vox_2'=4,'vox_3'=2,'load'=4] {'vox_2'}, use_global_device_ids=true, to_apply=%add.12 | all-reduce | flops 4 | bytes 32
  275.6 10.1 %all-reduce.14 = f32[4]{0:T(128)S(1)} all-reduce(f32[4]{0:T(128)S(1)} %dynamic-update-slice.14), channel_id=1, replica_groups=mesh['vox_0'=4,'vox_1'=2,'vox_2'=4,'vox_3'=2,'load'=4] {'load'}, use_global_device_ids=true, to_apply=%add.14 | all-reduce | flops 4 | bytes 32
  (116 shorter events, 56.5 us)
Async XLA Ops:
  0.6 18.5 %copy-start = (bf16[1024,512]{1,0:T(8,128)(2,1)S(1)}, bf16[1024,512]{1,0:T(8,128)(2,1)}, u32[]{:S(2)}) copy-start(bf16[1024,512]{1,0:T(8,128)(2,1)} %param.11) | copy-start | bytes 3145732
  2.1 9.5 %copy-start.4 = (f32[1024]{0:T(1024)S(1)}, f32[1024]{0:T(1024)}, u32[]{:S(2)}) copy-start(f32[1024]{0:T(1024)} %param.12) | copy-start | bytes 12292
  2.1 9.5 %copy-start.6 = (f32[1024]{0:T(1024)S(1)}, f32[1024]{0:T(1024)}, u32[]{:S(2)}) copy-start(f32[1024]{0:T(1024)} %param.13) | copy-start | bytes 12292
  2.1 17.0 %all-to-all-start = ((bf16[64,8,128]{2,1,0:T(8,128)(2,1)}), bf16[64,8,128]{2,1,0:T(8,128)(2,1)S(1)}, u32[]{:S(2)}, u32[]{:S(2)}) async-start(bf16[64,8,128]{2,1,0:T(8,128)(2,1)} %broadcast_in_dim.12), calls=%async_computation | async-start | bytes 262144 | tf_op jit(solution)/shard_map/all_to_all | solution.py:26
  11.6 7.5 %copy-start.5 = (f32[1024]{0:T(1024)S(1)}, f32[1024]{0:T(1024)}, u32[]{:S(2)}) copy-start(f32[1024]{0:T(1024)} %param.15) | copy-start | bytes 12292
  11.7 7.5 %copy-start.7 = (f32[128]{0:T(128)S(1)}, f32[128]{0:T(128)}, u32[]{:S(2)}) copy-start(f32[128]{0:T(128)} %param.16) | copy-start | bytes 1540
  11.7 9.0 %copy-start.8 = (s32[1024,128]{1,0:T(8,128)S(1)}, s32[1024,128]{1,0:T(8,128)}, u32[]{:S(2)}) copy-start(s32[1024,128]{1,0:T(8,128)} %param.17) | copy-start | bytes 1572868
  11.7 9.0 %copy-start.9 = (f32[1024]{0:T(1024)S(1)}, f32[1024]{0:T(1024)}, u32[]{:S(2)}) copy-start(f32[1024]{0:T(1024)} %param.14) | copy-start | bytes 12292
  22.3 14.4 %all-to-all-start.1 = ((f32[64,8,128]{2,1,0:T(8,128)}), f32[64,8,128]{2,1,0:T(8,128)S(1)}, u32[]{:S(2)}, u32[]{:S(2)}) async-start(f32[64,8,128]{2,1,0:T(8,128)} %bitcast.2), calls=%async_computation.1 | async-start | bytes 524288 | tf_op jit(solution)/shard_map/all_to_all | solution.py:42
  27.9 8.9 %copy-start.2 = (f32[8,128]{1,0:T(8,128)S(1)}, f32[8,128]{1,0:T(8,128)}, u32[]{:S(2)}) copy-start(f32[8,128]{1,0:T(8,128)} %param.20) | copy-start | bytes 12292
  37.5 5.7 %copy-start.14 = (u32[256]{0:T(256)S(1)}, u32[256]{0:T(256)}, u32[]{:S(2)}) copy-start(u32[256]{0:T(256)} %constant.41) | copy-start | bytes 3076
  37.5 17.6 %copy-start.13 = (u32[256]{0:T(256)S(1)}, u32[256]{0:T(256)}, u32[]{:S(2)}) copy-start(u32[256]{0:T(256)} %constant.46) | copy-start | bytes 3076
  37.6 29.1 %copy-start.12 = (u32[256]{0:T(256)S(1)}, u32[256]{0:T(256)}, u32[]{:S(2)}) copy-start(u32[256]{0:T(256)} %constant.51) | copy-start | bytes 3076
  37.6 36.6 %copy-start.11 = (u32[256]{0:T(256)S(1)}, u32[256]{0:T(256)}, u32[]{:S(2)}) copy-start(u32[256]{0:T(256)} %constant.56) | copy-start | bytes 3076
  37.6 48.1 %copy-start.10 = (u32[256]{0:T(256)S(1)}, u32[256]{0:T(256)}, u32[]{:S(2)}) copy-start(u32[256]{0:T(256)} %constant.61) | copy-start | bytes 3076
  37.6 68.4 %copy-start.3 = (f32[8,128]{1,0:T(8,128)S(1)}, f32[8,128]{1,0:T(8,128)}, u32[]{:S(2)}) copy-start(f32[8,128]{1,0:T(8,128)} %param.19) | copy-start | bytes 12292
  37.6 14.5 %all-to-all-start.2 = ((f32[64,8,128]{2,1,0:T(8,128)}), f32[64,8,128]{2,1,0:T(8,128)S(1)}, u32[]{:S(2)}, u32[]{:S(2)}) async-start(f32[64,8,128]{2,1,0:T(8,128)} %broadcast_in_dim.13), calls=%async_computation.2 | async-start | bytes 524288 | tf_op jit(solution)/shard_map/all_to_all | solution.py:26
  43.3 74.7 %copy-start.1 = (f32[1024,128]{1,0:T(8,128)S(1)}, f32[1024,128]{1,0:T(8,128)}, u32[]{:S(2)}) copy-start(f32[1024,128]{1,0:T(8,128)} %param.18) | copy-start | bytes 1572868
  118.6 0.8 copy-start.15
  134.5 73.8 %copy-start.16 = (f32[1024,128]{1,0:T(8,128)S(1)}, f32[1024,128]{1,0:T(8,128)}, u32[]{:S(2)}) copy-start(f32[1024,128]{1,0:T(8,128)} %copy-done.15) | copy-start | bytes 1572868
